TPU v7x, 32 devices: a whole 2x2x4 slice. The times are simulated.
32 devices in a mesh: gx: 4 (over y, x), gy: 4 (over z), gz: 2 (over core).
Axes of the slice: x: 2, y: 2, z: 4, core: 2. Of those that a mesh axis runs over, the one named last changes fastest.
Arguments:
- estimate: float32 [16, 256, 512], P('gz', 'gx', 'gy'), may hold values from 0.25 to 4
- view_data: float32 [16, 256, 512], P('gz', 'gx', 'gy'), may hold values from 0.25 to 4
- psf_stack: float32 [6, 31, 31, 31], replicated, may hold values from 0.01 to 1.53, as said below
- view_index: int32 [1], replicated, may hold values from 0 to 5
Outputs:
- updated_estimate: float32 [16, 256, 512], P('gz', 'gx', 'gy')
- level_one: float32 [8, 128, 256], P('gz', 'gx', 'gy')
- level_two: float32 [4, 64, 128], P('gz', 'gx', 'gy')
- level_three: float32 [2, 32, 64], P('gz', 'gx', 'gy')
- level_four: float32 [1, 16, 32], P(None, 'gx', 'gy')
- level_five: float32 [1, 8, 16], replicated
Inputs may be any that keep to these rules, and one draw needn't show every extreme that they name: `psf_stack`: every entry of every view's point spread function is positive.
All inputs are finite; a program needn't handle non-finite values.
Results may differ from a plain program's by a relative error of at most 0.000075.
Values sent between devices are 32-bit elements; how exact they have to be, the bound alone decides.
A program may use at most 128 MiB of HBM per device.

v0:
```python
import functools
import math

import jax
import jax.numpy as jnp
import numpy as np
from jax import lax
from jax.experimental import pallas as pl
from jax.experimental.pallas import tpu as pltpu
from jax.sharding import PartitionSpec as P

MESH = pl.DeviceIdType.MESH
BF = jnp.bfloat16
F32 = jnp.float32
LANES = 128
EDGE = 16
DIRECTIONS = ((1, 0), (-1, 0), (0, 1), (0, -1), (1, 1), (-1, 1), (1, -1), (-1, -1))


def two_parts(matrix):
    matrix = np.asarray(matrix, np.float32)
    high = matrix.astype(BF)
    low = (matrix - high.astype(np.float32)).astype(BF)
    return high, low


def split(x):
    high = x.astype(BF)
    return high, (x - high.astype(F32)).astype(BF)


def dot(a, b):
    return jnp.dot(a, b, preferred_element_type=F32)


def tables(nx, ny, extent):
    radius = (extent - 1) // 2
    lx, ly = nx + 2 * EDGE, ny + 2 * EDGE
    nf = ly // 2 + 1
    freq_y = np.arange(nf)
    freq_x = np.arange(lx)

    def wave(k, n, length):
        return 2 * math.pi / length * np.mod(np.outer(k, n), length)

    pos = np.concatenate([EDGE + np.arange(ny), np.arange(EDGE), EDGE + ny + np.arange(EDGE)])
    fy = np.zeros((ny + LANES, 2 * LANES))
    angle = wave(pos, freq_y, ly)
    fy[: pos.size, :nf] = np.cos(angle)
    fy[: pos.size, LANES : LANES + nf] = -np.sin(angle)
    ky = np.zeros((LANES, 2 * LANES))
    angle = wave(np.arange(extent) - radius, freq_y, ly)
    ky[:extent, :nf] = np.cos(angle)
    ky[:extent, LANES : LANES + nf] = -np.sin(angle)
    iy = np.zeros((2 * LANES, ny))
    weight = np.full((nf, 1), 2.0)
    weight[0] = weight[-1] = 1.0
    angle = wave(freq_y, EDGE + np.arange(ny), ly)
    iy[:nf] = weight / ly * np.cos(angle)
    iy[LANES : LANES + nf] = -weight / ly * np.sin(angle)

    angle = wave(freq_x, np.arange(lx), lx)
    fx = np.block([[np.cos(angle), np.sin(angle)], [-np.sin(angle), np.cos(angle)]])
    angle = wave(EDGE + np.arange(nx), freq_x, lx)
    ix = np.block([[np.cos(angle), -np.sin(angle)], [np.sin(angle), np.cos(angle)]]) / lx
    kx = np.zeros((2 * lx, 2, extent + 1))
    angle = wave(freq_x, np.arange(extent) - radius, lx)
    kx[:lx, 0, :extent] = np.cos(angle)
    kx[:lx, 1, :extent] = np.sin(angle)
    kx[lx:, 0, :extent] = -np.sin(angle)
    kx[lx:, 1, :extent] = np.cos(angle)
    kx = kx.reshape(2 * lx, 2 * (extent + 1))

    fy_hi, fy_lo = two_parts(fy)
    ky_hi, ky_lo = two_parts(ky)
    iy_hi, iy_lo = two_parts(iy)
    fx_hi, fx_lo = two_parts(fx)
    ix_hi, ix_lo = two_parts(ix)
    kx_hi, kx_lo = two_parts(kx)

    py = np.zeros((ny, LANES))
    px = np.zeros((nx, nx))
    row, col = 0, 0
    places = []
    for level in range(1, 6):
        size = 2**level
        rows, cols = nx // size, ny // size
        places.append((row, rows, col, cols))
        for r in range(rows):
            px[row + r, r * size : (r + 1) * size] = 1.0 / size
        for c in range(cols):
            py[c * size : (c + 1) * size, col + c] = 1.0 / size
        row, col = row + rows, col + cols
    arrays = (
        fy_hi,
        fy_lo,
        np.concatenate([fx_hi, fx_lo], 0),
        ky_hi,
        ky_lo,
        np.concatenate([kx_hi, kx_hi, kx_lo], 1),
        np.concatenate([ix_hi, ix_lo], 0),
        iy_hi,
        iy_lo,
        py.astype(BF),
        px.astype(BF),
    )
    return arrays, tuple(places)


def kernel(
    sizes,
    places,
    index_ref, est_ref, view_ref, psf_hbm,
    fy_hi, fy_lo, fx2, ky_hi, ky_lo, kx3, ix2, iy_hi, iy_lo, py, px,
    out_ref, one_ref, two_ref, three_ref, four_ref, five_ref,
    psf, psf_pad, kd, k2, a_hi, a_lo, d_hi, d_lo, own, peer, mix, ratio,
    pack, xhalo, yhalo, share, share_in, tiles,
    psf_sem, hs, hr, es, er, ps, pr, gs, gr,
):
    gxn, gyn = sizes
    nz, nx, ny = est_ref.shape
    extent = psf_hbm.shape[1]
    lx = nx + 2 * EDGE
    gx, gy, gz = lax.axis_index("gx"), lax.axis_index("gy"), lax.axis_index("gz")
    partner = {"gx": gx, "gy": gy, "gz": 1 - gz}
    chips = gxn * gyn

    psf_copy = pltpu.make_async_copy(psf_hbm, psf, psf_sem)
    psf_copy.start()

    def chip_at(offset):
        x = lax.rem(gx + offset // gyn, gxn)
        y = lax.rem(gy + lax.rem(offset, gyn), gyn)
        return {"gx": x, "gy": y, "gz": gz}

    barrier = pltpu.get_barrier_semaphore()
    pl.semaphore_signal(barrier, inc=1, device_id=partner, device_id_type=MESH)

    @pl.loop(1, chips)
    def _(offset):
        pl.semaphore_signal(barrier, inc=1, device_id=chip_at(offset), device_id_type=MESH)

    def exists(dx, dy):
        ok = None
        for c, n, d in ((gx, gxn, dx), (gy, gyn, dy)):
            if d > 0:
                t = c < n - 1
            elif d < 0:
                t = c > 0
            else:
                continue
            ok = t if ok is None else jnp.logical_and(ok, t)
        return ok

    def halo_parts(phase, field, dx, dy):
        if dy == 0:
            rows = slice(nx - EDGE, nx) if dx > 0 else slice(0, EDGE)
            return field.at[:, rows, :], xhalo.at[phase, 0 if dx > 0 else 1]
        side = 0 if dy > 0 else 1
        if dx == 0:
            return pack.at[phase, side], yhalo.at[phase, side, pl.ds(EDGE, nx), :]
        rows = pl.ds(nx - EDGE, EDGE) if dx > 0 else pl.ds(0, EDGE)
        to = pl.ds(0, EDGE) if dx > 0 else pl.ds(EDGE + nx, EDGE)
        return pack.at[phase, side, rows, :], yhalo.at[phase, side, to, :]

    def halo_copy(phase, field, d):
        dx, dy = DIRECTIONS[d]
        source, target = halo_parts(phase, field, dx, dy)
        return pltpu.make_async_remote_copy(
            src_ref=source,
            dst_ref=target,
            send_sem=hs.at[phase, d],
            recv_sem=hr.at[phase, d],
            device_id={"gx": gx + dx, "gy": gy + dy, "gz": gz},
            device_id_type=MESH,
        )

    def do_pack(phase, field):
        lane = lax.broadcasted_iota(jnp.int32, (nx, LANES), 1) // EDGE
        last = jnp.zeros((nx, LANES), F32)
        first = jnp.zeros((nx, LANES), F32)
        for z in range(nz):
            plane = field[z]
            last = jnp.where(lane == z, pltpu.roll(plane, (EDGE * z + EDGE) % LANES, 1), last)
            first = jnp.where(lane == z, pltpu.roll(plane, EDGE * z, 1) if z else plane, first)
        pack[phase, 0] = last
        pack[phase, 1] = first

    def zero_missing(phase):
        for d, (dx, dy) in enumerate(DIRECTIONS):
            target = halo_parts(phase, est_ref, dx, dy)[1]

            @pl.when(jnp.logical_not(exists(-dx, -dy)))
            def _():
                target[...] = jnp.zeros(target.shape, F32)

    def send_halos(phase, field):
        for d, (dx, dy) in enumerate(DIRECTIONS):

            @pl.when(exists(dx, dy))
            def _():
                halo_copy(phase, field, d).start()

    def wait_halos(phase, field):
        for d, (dx, dy) in enumerate(DIRECTIONS):

            @pl.when(exists(-dx, -dy))
            def _():
                halo_copy(phase, field, d).wait_recv()

    def wait_sends(phase, field):
        for d, (dx, dy) in enumerate(DIRECTIONS):

            @pl.when(exists(dx, dy))
            def _():
                halo_copy(phase, field, d).wait_send()

    def plane_copy(phase, z):
        return pltpu.make_async_remote_copy(
            src_ref=own.at[phase, z],
            dst_ref=peer.at[phase, z],
            send_sem=es.at[phase, z],
            recv_sem=er.at[phase, z],
            device_id=partner,
            device_id_type=MESH,
        )

    def forward(phase, field):
        lane = lax.broadcasted_iota(jnp.int32, (lx, LANES), 1)
        for z in range(nz):
            body = jnp.concatenate([xhalo[phase, 0, z], field[z], xhalo[phase, 1, z]], axis=0)
            left, right = yhalo[phase, 0], yhalo[phase, 1]
            if z:
                left = pltpu.roll(left, LANES - EDGE * z, 1)
            if z != 1:
                right = pltpu.roll(right, (EDGE - EDGE * z) % LANES, 1)
            side = jnp.where(lane < EDGE, left, jnp.where(lane < 2 * EDGE, right, 0.0))
            full = jnp.concatenate([body, side], axis=1)
            a_hi[z], a_lo[z] = split(full)
        for z in range(nz):
            hi = a_hi[z]
            x1 = dot(hi, fy_hi[...]) + dot(a_lo[z], fy_hi[...]) + dot(hi, fy_lo[...])
            hi, lo = split(x1)
            d_hi[z, pl.ds(0, lx), :] = hi[:, :LANES]
            d_hi[z, pl.ds(lx, lx), :] = hi[:, LANES:]
            d_lo[z, pl.ds(0, lx), :] = lo[:, :LANES]
            d_lo[z, pl.ds(lx, lx), :] = lo[:, LANES:]
        for z in range(0, nz, 2):
            hi = jnp.concatenate([d_hi[z], d_hi[z + 1]], axis=1)
            lo = jnp.concatenate([d_lo[z], d_lo[z + 1]], axis=1)
            both = dot(fx2[...], hi)
            x2 = both[: 2 * lx] + both[2 * lx :] + dot(fx2[pl.ds(0, 2 * lx), :], lo)
            own[phase, z] = x2[:, :LANES]
            own[phase, z + 1] = x2[:, LANES:]
            plane_copy(phase, z).start()
            plane_copy(phase, z + 1).start()

    def mix_planes(source, phase, base, conj, add):
        @pl.loop(0, lx // 8)
        def _(s):
            re = pl.ds(pl.multiple_of(s * 8, 8), 8)
            im = pl.ds(pl.multiple_of(lx + s * 8, 8), 8)
            vr = [source[phase, j, re, :] for j in range(nz)]
            vi = [source[phase, j, im, :] for j in range(nz)]
            kr, ki = {}, {}
            for d in range(1 - nz, nz):
                kr[d] = k2[base + d, re, :]
                ki[d] = k2[base + d, im, :]
            for i in range(nz):
                yr = mix[i, re, :] if add else None
                yi = mix[i, im, :] if add else None
                for j in range(nz):
                    d = j - i if conj else i - j
                    rr, ii = kr[d] * vr[j], ki[d] * vi[j]
                    ri, ir = kr[d] * vi[j], ki[d] * vr[j]
                    tr, ti = (rr + ii, ri - ir) if conj else (rr - ii, ri + ir)
                    yr = tr if yr is None else yr + tr
                    yi = ti if yi is None else yi + ti
                mix[i, re, :] = yr
                mix[i, im, :] = yi

    def inverse(write):
        for z in range(0, nz, 2):
            y = jnp.concatenate([mix[z], mix[z + 1]], axis=1)
            hi, lo = split(y)
            both = dot(ix2[...], hi)
            g = both[: 2 * nx] + both[2 * nx :] + dot(ix2[pl.ds(0, 2 * nx), :], lo)
            for k in range(2):
                part = g[:, k * LANES : (k + 1) * LANES]
                rows = jnp.concatenate([part[:nx], part[nx:]], axis=1)
                hi, lo = split(rows)
                write(
                    z + k,
                    dot(hi, iy_hi[...]) + dot(lo, iy_hi[...]) + dot(hi, iy_lo[...]),
                )

    def convolve(phase, field, conj, write):
        forward(phase, field)
        sign = 1 - 2 * gz if conj else 2 * gz - 1
        middle = (extent - 1) // 2
        mix_planes(own, phase, middle, conj, False)
        for z in range(nz):
            plane_copy(phase, z).wait_recv()
        mix_planes(peer, phase, middle + sign * nz, conj, True)
        inverse(write)

    do_pack(0, est_ref)
    zero_missing(0)
    pl.semaphore_wait(barrier, chips)
    send_halos(0, est_ref)
    zero_missing(1)

    psf_copy.wait()
    chosen = psf[index_ref[0]]
    total = jnp.sum(chosen, axis=0)
    total = jnp.sum(jnp.sum(total, axis=1, keepdims=True), axis=0, keepdims=True)
    psf_pad[...] = jnp.zeros(psf_pad.shape, F32)
    psf_pad[pl.ds(0, extent), pl.ds(0, extent), pl.ds(0, extent)] = chosen * (1.0 / total)[None]
    wide = extent + 1

    @pl.loop(0, wide // 4)
    def _(q):
        block = psf_pad[pl.ds(q * 4, 4)].reshape(4 * wide, LANES)
        hi, lo = split(block)
        x1 = dot(hi, ky_hi[...]) + dot(lo, ky_hi[...]) + dot(hi, ky_lo[...])
        hi, lo = split(x1)
        hi = hi.reshape(4, wide, 2 * LANES)
        lo = lo.reshape(4, wide, 2 * LANES)
        for n, part in enumerate((hi, lo, hi)):
            kd[pl.ds(q * 4, 4), pl.ds(2 * n * wide, wide), :] = part[:, :, :LANES]
            kd[pl.ds(q * 4, 4), pl.ds(2 * n * wide + wide, wide), :] = part[:, :, LANES:]

    @pl.loop(0, wide // 4)
    def _(q):
        for h in range(2):
            n = q * 4 + 2 * h
            pair = jnp.concatenate([kd[n], kd[n + 1]], axis=1)
            spectrum = dot(kx3[...], pair)
            k2[n] = spectrum[:, :LANES]
            k2[n + 1] = spectrum[:, LANES:]

    wait_halos(0, est_ref)

    def write_ratio(z, blurred):
        ratio[z] = view_ref[z] / blurred

    convolve(0, est_ref, False, write_ratio)

    do_pack(1, ratio)
    send_halos(1, ratio)
    wait_halos(1, ratio)

    def write_update(z, correction):
        out_ref[z] = est_ref[z] * correction

    convolve(1, ratio, True, write_update)

    halves = [(out_ref[2 * i] + out_ref[2 * i + 1]) * 0.5 for i in range(nz // 2)]
    quarters = [(halves[2 * i] + halves[2 * i + 1]) * 0.5 for i in range(nz // 4)]
    eighth = (quarters[0] + quarters[1]) * 0.5

    def pooled(plane):
        hi, lo = split(plane)
        t = dot(hi, py[...]) + dot(lo, py[...])
        hi, lo = split(t)
        return dot(px[...], hi) + dot(px[...], lo)

    r4, c4 = places[3][0], places[3][2]
    last = pooled(eighth)
    share[0] = last[r4 : r4 + 8]
    share_copy = pltpu.make_async_remote_copy(
        src_ref=share.at[0], dst_ref=share_in, send_sem=ps, recv_sem=pr,
        device_id=partner, device_id_type=MESH,
    )
    share_copy.start()
    row, rows, col, cols = places[2]
    three_ref[0] = last[row : row + rows, col : col + cols]
    row, rows, col, cols = places[0]
    for i, plane in enumerate(halves):
        one_ref[i] = pooled(plane)[row : row + rows, col : col + cols]
    row, rows, col, cols = places[1]
    for i, plane in enumerate(quarters):
        two_ref[i] = pooled(plane)[row : row + rows, col : col + cols]
    share_copy.wait()
    both = (share[0] + share_in[...]) * 0.5
    four_ref[0] = both[: places[3][1], c4 : c4 + places[3][3]]
    row, rows, col, cols = places[4]
    row = row - r4
    r = lax.broadcasted_iota(jnp.int32, both.shape, 0)
    c = lax.broadcasted_iota(jnp.int32, both.shape, 1)
    inside = (r >= row) & (r < row + rows) & (c >= col) & (c < col + cols)
    mine = jnp.where(inside, both, 0.0)
    height = tiles.shape[1]
    if height > 8:
        mine = jnp.concatenate([mine, jnp.zeros((height - 8, LANES), F32)], axis=0)
    mine = pltpu.roll(mine, lax.rem(gy * cols + LANES - col, LANES), 1)
    mine = pltpu.roll(mine, lax.rem(gx * rows + height - row, height), 0)
    tiles[0] = mine

    def tile_copy(offset):
        return pltpu.make_async_remote_copy(
            src_ref=tiles.at[0], dst_ref=tiles.at[offset],
            send_sem=gs.at[offset], recv_sem=gr.at[offset],
            device_id=chip_at(offset), device_id_type=MESH,
        )

    @pl.loop(1, chips)
    def _(offset):
        tile_copy(offset).start()

    for phase, field in ((0, est_ref), (1, ratio)):
        wait_sends(phase, field)
        for z in range(nz):
            plane_copy(phase, z).wait_send()

    @pl.loop(1, chips)
    def _(offset):
        tile_copy(offset).wait()

    five = tiles[0]
    for offset in range(1, chips):
        five = five + tiles[offset]
    five_ref[0] = five[: five_ref.shape[1], : five_ref.shape[2]]


def local(sizes, estimate, view_data, psf_stack, view_index):
    gxn, gyn = sizes
    nz, nx, ny = estimate.shape
    views, extent = psf_stack.shape[:2]
    arrays, places = tables(nx, ny, extent)
    lx = nx + 2 * EDGE
    wide = extent + 1
    chips = gxn * gyn
    vmem = pl.BlockSpec(memory_space=pltpu.VMEM)

    def shape(*dims):
        return jax.ShapeDtypeStruct(dims, F32)

    rows5, cols5 = places[4][1] * gxn, places[4][3] * gyn
    dma = pltpu.SemaphoreType.DMA
    return pl.pallas_call(
        functools.partial(kernel, sizes, places),
        out_shape=(
            shape(nz, nx, ny),
            shape(nz // 2, nx // 2, ny // 2),
            shape(nz // 4, nx // 4, ny // 4),
            shape(nz // 8, nx // 8, ny // 8),
            shape(1, nx // 16, ny // 16),
            shape(1, rows5, cols5),
        ),
        in_specs=[pl.BlockSpec(memory_space=pltpu.SMEM), vmem, vmem, pl.BlockSpec(memory_space=pl.ANY)]
        + [vmem] * len(arrays),
        out_specs=(vmem,) * 6,
        scratch_shapes=[
            pltpu.VMEM(psf_stack.shape, F32),
            pltpu.VMEM((wide, wide, LANES), F32),
            pltpu.VMEM((wide, 6 * wide, LANES), BF),
            pltpu.VMEM((wide, 2 * lx, LANES), F32),
            pltpu.VMEM((nz, lx, 2 * LANES), BF),
            pltpu.VMEM((nz, lx, 2 * LANES), BF),
            pltpu.VMEM((nz, 2 * lx, LANES), BF),
            pltpu.VMEM((nz, 2 * lx, LANES), BF),
            pltpu.VMEM((2, nz, 2 * lx, LANES), F32),
            pltpu.VMEM((2, nz, 2 * lx, LANES), F32),
            pltpu.VMEM((nz, 2 * lx, LANES), F32),
            pltpu.VMEM((nz, nx, ny), F32),
            pltpu.VMEM((2, 2, nx, LANES), F32),
            pltpu.VMEM((2, 2, nz, EDGE, ny), F32),
            pltpu.VMEM((2, 2, lx, LANES), F32),
            pltpu.VMEM((1, 8, LANES), F32),
            pltpu.VMEM((8, LANES), F32),
            pltpu.VMEM((chips, max(8, rows5), LANES), F32),
            dma,
            dma((2, 8)),
            dma((2, 8)),
            dma((2, nz)),
            dma((2, nz)),
            dma,
            dma,
            dma((chips,)),
            dma((chips,)),
        ],
        compiler_params=pltpu.CompilerParams(
            collective_id=0, has_side_effects=True, vmem_limit_bytes=48 * 1024 * 1024
        ),
        name="deconvolve",
    )(view_index, estimate, view_data, psf_stack, *[jnp.asarray(a) for a in arrays])


def solution(mesh):
    return jax.shard_map(
        functools.partial(local, (mesh.shape["gx"], mesh.shape["gy"])),
        mesh=mesh,
        in_specs=(P("gz", "gx", "gy"), P("gz", "gx", "gy"), P(), P()),
        out_specs=(
            P("gz", "gx", "gy"),
            P("gz", "gx", "gy"),
            P("gz", "gx", "gy"),
            P("gz", "gx", "gy"),
            P(None, "gx", "gy"),
            P(),
        ),
        check_vma=False,
    )
```

profile of v0, /device:TPU:0, one launch (start us, length us, event | category | flops | bytes accessed | tf_op | source)
XLA Modules:
  0.0 51.4 jit_solution(17496998456502816028)
XLA Ops:
  1.3 0.0 copy-start
  1.3 1.9 %copy-done = f32[6,31,31,31]{3,2,1,0:T(8,128)S(1)} copy-done((f32[6,31,31,31]{3,2,1,0:T(8,128)S(1)}, f32[6,31,31,31]{3,2,1,0:T(8,128)}, u32[]{:S(2)}) %copy-start) | copy-done | bytes 715008
  3.1 0.0 copy-start.1
  3.1 0.9 %copy-done.1 = f32[8,64,128]{2,1,0:T(8,128)S(1)} copy-done((f32[8,64,128]{2,1,0:T(8,128)S(1)}, f32[8,64,128]{2,1,0:T(8,128)}, u32[]{:S(2)}) %copy-start.1) | copy-done | bytes 262168
  4.1 0.0 copy-start.2
  4.1 0.9 %copy-done.2 = f32[8,64,128]{2,1,0:T(8,128)S(1)} copy-done((f32[8,64,128]{2,1,0:T(8,128)S(1)}, f32[8,64,128]{2,1,0:T(8,128)}, u32[]{:S(2)}) %copy-start.2) | copy-done | bytes 262168
  5.0 0.0 copy-start.3
  5.0 0.9 %copy-done.3 = bf16[384,192]{1,0:T(8,128)(2,1)S(1)} copy-done((bf16[384,192]{1,0:T(8,128)(2,1)S(1)}, bf16[384,192]{1,0:T(8,128)(2,1)}, u32[]{:S(2)}) %copy-start.3) | copy-done | bytes 147480
  6.0 0.0 copy-start.4
  6.0 0.9 %copy-done.4 = bf16[256,192]{1,0:T(8,128)(2,1)S(1)} copy-done((bf16[256,192]{1,0:T(8,128)(2,1)S(1)}, bf16[256,192]{1,0:T(8,128)(2,1)}, u32[]{:S(2)}) %copy-start.4) | copy-done | bytes 98328
  6.9 0.0 copy-start.5
  6.9 0.9 %copy-done.5 = bf16[256,256]{1,0:T(8,128)(2,1)S(1)} copy-done((bf16[256,256]{1,0:T(8,128)(2,1)S(1)}, bf16[256,256]{1,0:T(8,128)(2,1)}, u32[]{:S(2)}) %copy-start.5) | copy-done | bytes 131096
  7.8 0.0 copy-start.6
  7.8 0.9 %copy-done.6 = bf16[256,256]{1,0:T(8,128)(2,1)S(1)} copy-done((bf16[256,256]{1,0:T(8,128)(2,1)S(1)}, bf16[256,256]{1,0:T(8,128)(2,1)}, u32[]{:S(2)}) %copy-start.6) | copy-done | bytes 131096
  8.7 0.0 copy-start.7
  8.7 0.9 %copy-done.7 = bf16[192,192]{1,0:T(8,128)(2,1)S(1)} copy-done((bf16[192,192]{1,0:T(8,128)(2,1)S(1)}, bf16[192,192]{1,0:T(8,128)(2,1)}, u32[]{:S(2)}) %copy-start.7) | copy-done | bytes 73752
  9.6 0.0 copy-start.8
  9.6 0.8 %copy-done.8 = bf16[256,128]{1,0:T(8,128)(2,1)S(1)} copy-done((bf16[256,128]{1,0:T(8,128)(2,1)S(1)}, bf16[256,128]{1,0:T(8,128)(2,1)}, u32[]{:S(2)}) %copy-start.8) | copy-done | bytes 65560
  10.4 0.0 copy-start.9
  10.4 0.8 %copy-done.9 = bf16[256,128]{1,0:T(8,128)(2,1)S(1)} copy-done((bf16[256,128]{1,0:T(8,128)(2,1)S(1)}, bf16[256,128]{1,0:T(8,128)(2,1)}, u32[]{:S(2)}) %copy-start.9) | copy-done | bytes 65560
  11.3 0.0 copy-start.10
  11.3 0.8 %copy-done.10 = bf16[128,256]{1,0:T(8,128)(2,1)S(1)} copy-done((bf16[128,256]{1,0:T(8,128)(2,1)S(1)}, bf16[128,256]{1,0:T(8,128)(2,1)}, u32[]{:S(2)}) %copy-start.10) | copy-done | bytes 65560
  12.1 0.0 copy-start.11
  12.1 0.8 %copy-done.11 = bf16[128,256]{1,0:T(8,128)(2,1)S(1)} copy-done((bf16[128,256]{1,0:T(8,128)(2,1)S(1)}, bf16[128,256]{1,0:T(8,128)(2,1)}, u32[]{:S(2)}) %copy-start.11) | copy-done | bytes 65560
  12.9 0.0 copy-start.12
  12.9 0.8 %copy-done.12 = bf16[128,128]{1,0:T(8,128)(2,1)S(1)} copy-done((bf16[128,128]{1,0:T(8,128)(2,1)S(1)}, bf16[128,128]{1,0:T(8,128)(2,1)}, u32[]{:S(2)}) %copy-start.12) | copy-done | bytes 32792
  13.7 0.0 copy-start.13
  13.7 0.7 %copy-done.13 = bf16[64,64]{1,0:T(8,128)(2,1)S(1)} copy-done((bf16[64,64]{1,0:T(8,128)(2,1)S(1)}, bf16[64,64]{1,0:T(8,128)(2,1)}, u32[]{:S(2)}) %copy-start.13) | copy-done | bytes 8216
  14.4 33.2 %deconvolve.1 = (f32[8,64,128]{2,1,0:T(8,128)S(1)}, f32[4,32,64]{2,1,0:T(8,128)S(1)}, f32[2,16,32]{2,1,0:T(8,128)S(1)}, f32[1,8,16]{2,1,0:T(8,128)S(1)}, f32[1,4...) custom-call(s32[1]{0:T(128)S(6)} %copy.27.index_ref, f32[8,64,128]{2,1,0:T(8,128)S(1)} %copy-done.1, ...), custom_call_target="tpu_custom_call" | custom-call | tf_op jit(solution)/shard_map/deconvolve/pallas_call | solution.py:441
  47.7 0.7 %copy.28 = f32[8,64,128]{2,1,0:T(8,128)} copy(f32[8,64,128]{2,1,0:T(8,128)S(1)} %get-tuple-element.12) | data formatting | bytes 524288
  48.4 0.6 %copy.29 = f32[4,32,64]{2,1,0:T(8,128)} copy(f32[4,32,64]{2,1,0:T(8,128)S(1)} %get-tuple-element.13) | data formatting | bytes 65536
  49.0 0.6 %copy.30 = f32[2,16,32]{2,1,0:T(8,128)} copy(f32[2,16,32]{2,1,0:T(8,128)S(1)} %get-tuple-element.14) | data formatting | bytes 8192
  49.6 0.6 %copy.31 = f32[1,8,16]{2,1,0:T(8,128)} copy(f32[1,8,16]{2,1,0:T(8,128)S(1)} %get-tuple-element.15) | data formatting | bytes 1024
  50.2 0.6 %copy.32 = f32[1,4,8]{2,1,0:T(4,128)} copy(f32[1,4,8]{2,1,0:T(4,128)S(1)} %get-tuple-element.16) | data formatting | bytes 256
  50.8 0.6 %copy.33 = f32[1,8,16]{2,1,0:T(8,128)} copy(f32[1,8,16]{2,1,0:T(8,128)S(1)} %get-tuple-element.17) | data formatting | bytes 1024
Async XLA Ops:
  1.3 1.9 %copy-start = (f32[6,31,31,31]{3,2,1,0:T(8,128)S(1)}, f32[6,31,31,31]{3,2,1,0:T(8,128)}, u32[]{:S(2)}) copy-start(f32[6,31,31,31]{3,2,1,0:T(8,128)} %psf_hbm.1) | copy-start | bytes 2144956
  3.1 0.9 %copy-start.1 = (f32[8,64,128]{2,1,0:T(8,128)S(1)}, f32[8,64,128]{2,1,0:T(8,128)}, u32[]{:S(2)}) copy-start(f32[8,64,128]{2,1,0:T(8,128)} %est_ref.1) | copy-start | bytes 786436
  4.1 0.9 %copy-start.2 = (f32[8,64,128]{2,1,0:T(8,128)S(1)}, f32[8,64,128]{2,1,0:T(8,128)}, u32[]{:S(2)}) copy-start(f32[8,64,128]{2,1,0:T(8,128)} %view_ref.1) | copy-start | bytes 786436
  5.0 0.9 %copy-start.3 = (bf16[384,192]{1,0:T(8,128)(2,1)S(1)}, bf16[384,192]{1,0:T(8,128)(2,1)}, u32[]{:S(2)}) copy-start(bf16[384,192]{1,0:T(8,128)(2,1)} %constant.24.clone.fx2) | copy-start | bytes 442372
  6.0 0.9 %copy-start.4 = (bf16[256,192]{1,0:T(8,128)(2,1)S(1)}, bf16[256,192]{1,0:T(8,128)(2,1)}, u32[]{:S(2)}) copy-start(bf16[256,192]{1,0:T(8,128)(2,1)} %constant.28.clone.ix2) | copy-start | bytes 294916
  6.9 0.9 %copy-start.5 = (bf16[256,256]{1,0:T(8,128)(2,1)S(1)}, bf16[256,256]{1,0:T(8,128)(2,1)}, u32[]{:S(2)}) copy-start(bf16[256,256]{1,0:T(8,128)(2,1)} %constant.23.clone.fy_lo) | copy-start | bytes 393220
  7.8 0.9 %copy-start.6 = (bf16[256,256]{1,0:T(8,128)(2,1)S(1)}, bf16[256,256]{1,0:T(8,128)(2,1)}, u32[]{:S(2)}) copy-start(bf16[256,256]{1,0:T(8,128)(2,1)} %constant.22.clone.fy_hi) | copy-start | bytes 393220
  8.7 0.9 %copy-start.7 = (bf16[192,192]{1,0:T(8,128)(2,1)S(1)}, bf16[192,192]{1,0:T(8,128)(2,1)}, u32[]{:S(2)}) copy-start(bf16[192,192]{1,0:T(8,128)(2,1)} %constant.27.clone.kx3) | copy-start | bytes 221188
  9.6 0.8 %copy-start.8 = (bf16[256,128]{1,0:T(8,128)(2,1)S(1)}, bf16[256,128]{1,0:T(8,128)(2,1)}, u32[]{:S(2)}) copy-start(bf16[256,128]{1,0:T(8,128)(2,1)} %constant.30.clone.iy_lo) | copy-start | bytes 196612
  10.4 0.8 %copy-start.9 = (bf16[256,128]{1,0:T(8,128)(2,1)S(1)}, bf16[256,128]{1,0:T(8,128)(2,1)}, u32[]{:S(2)}) copy-start(bf16[256,128]{1,0:T(8,128)(2,1)} %constant.29.clone.iy_hi) | copy-start | bytes 196612
  11.3 0.8 %copy-start.10 = (bf16[128,256]{1,0:T(8,128)(2,1)S(1)}, bf16[128,256]{1,0:T(8,128)(2,1)}, u32[]{:S(2)}) copy-start(bf16[128,256]{1,0:T(8,128)(2,1)} %constant.26.clone.ky_lo) | copy-start | bytes 196612
  12.1 0.8 %copy-start.11 = (bf16[128,256]{1,0:T(8,128)(2,1)S(1)}, bf16[128,256]{1,0:T(8,128)(2,1)}, u32[]{:S(2)}) copy-start(bf16[128,256]{1,0:T(8,128)(2,1)} %constant.25.clone.ky_hi) | copy-start | bytes 196612
  12.9 0.8 %copy-start.12 = (bf16[128,128]{1,0:T(8,128)(2,1)S(1)}, bf16[128,128]{1,0:T(8,128)(2,1)}, u32[]{:S(2)}) copy-start(bf16[128,128]{1,0:T(8,128)(2,1)} %constant.31.clone.py) | copy-start | bytes 98308
  13.7 0.7 %copy-start.13 = (bf16[64,64]{1,0:T(8,128)(2,1)S(1)}, bf16[64,64]{1,0:T(8,128)(2,1)}, u32[]{:S(2)}) copy-start(bf16[64,64]{1,0:T(8,128)(2,1)} %constant.32.clone.px) | copy-start | bytes 24580
where the time goes:
time: 52 us; the launch traced here: 51.4 us
  Pallas kernels  33.2 us (64%)
  local copies, waits for them, and re-layouts  16.8 us (32%)
  between operations  1.31 us (3%)
    pallas_call x1, Pallas kernels, local(): pl.pallas_call(functools.partial(kernel, sizes, places), out_shape=(shape...  33.2 us
    unnamed x34, local copies, waits for them, and re-layouts  16.8 us

commit v1 on v0

--- a/solution.py
+++ b/solution.py
@@ -14,6 +14,7 @@
 F32 = jnp.float32
 LANES = 128
 EDGE = 16
+TABLES = 11
 DIRECTIONS = ((1, 0), (-1, 0), (0, 1), (0, -1), (1, 1), (-1, 1), (1, -1), (-1, -1))
 
 
@@ -110,23 +111,42 @@
 def kernel(
     sizes,
     places,
-    index_ref, est_ref, view_ref, psf_hbm,
-    fy_hi, fy_lo, fx2, ky_hi, ky_lo, kx3, ix2, iy_hi, iy_lo, py, px,
+    index_ref, est_hbm, view_hbm, psf_hbm, *rest,
+):
+    count = TABLES
+    tables_hbm, rest = rest[:count], rest[count:]
+    body(
+        sizes, places, index_ref, (est_hbm, psf_hbm, *tables_hbm, view_hbm), *rest
+    )
+
+
+def body(
+    sizes,
+    places,
+    index_ref, operands,
     out_ref, one_ref, two_ref, three_ref, four_ref, five_ref,
-    psf, psf_pad, kd, k2, a_hi, a_lo, d_hi, d_lo, own, peer, mix, ratio,
+    psf_pad, kd, k2, own, peer, mix, ratio,
     pack, xhalo, yhalo, share, share_in, tiles,
-    psf_sem, hs, hr, es, er, ps, pr, gs, gr,
+    in_sem, xs, xr, hs, hr, es, er, ps, pr, gs, gr,
+    est_ref, psf, fy_hi, fy_lo, fx2, ky_hi, ky_lo, kx3, ix2, iy_hi, iy_lo, py, px, view_ref,
 ):
     gxn, gyn = sizes
     nz, nx, ny = est_ref.shape
-    extent = psf_hbm.shape[1]
+    extent = psf.shape[1]
+    pairs = nz // 2
     lx = nx + 2 * EDGE
     gx, gy, gz = lax.axis_index("gx"), lax.axis_index("gy"), lax.axis_index("gz")
     partner = {"gx": gx, "gy": gy, "gz": 1 - gz}
     chips = gxn * gyn
 
-    psf_copy = pltpu.make_async_copy(psf_hbm, psf, psf_sem)
-    psf_copy.start()
+    resident = (
+        est_ref, psf, fy_hi, fy_lo, fx2, ky_hi, ky_lo, kx3, ix2, iy_hi, iy_lo, py, px, view_ref
+    )
+    loads = [
+        pltpu.make_async_copy(a, b, in_sem.at[i])
+        for i, (a, b) in enumerate(zip(operands, resident))
+    ]
+    loads[0].start()
 
     def chip_at(offset):
         x = lax.rem(gx + offset // gyn, gxn)
@@ -139,6 +159,9 @@
     @pl.loop(1, chips)
     def _(offset):
         pl.semaphore_signal(barrier, inc=1, device_id=chip_at(offset), device_id_type=MESH)
+
+    for load in loads[1:]:
+        load.start()
 
     def exists(dx, dy):
         ok = None
@@ -175,6 +198,33 @@
             device_id_type=MESH,
         )
 
+    def pair_copy(phase, field, d, q):
+        source, target = halo_parts(phase, field, *DIRECTIONS[d])
+        planes = pl.ds(2 * q, 2)
+        rows = pl.ds(nx - EDGE, EDGE) if d == 0 else pl.ds(0, EDGE)
+        return pltpu.make_async_remote_copy(
+            src_ref=field.at[planes, rows, :],
+            dst_ref=xhalo.at[phase, d, planes],
+            send_sem=xs.at[phase, d, q],
+            recv_sem=xr.at[phase, d, q],
+            device_id={"gx": gx + DIRECTIONS[d][0], "gy": gy, "gz": gz},
+            device_id_type=MESH,
+        )
+
+    def for_existing(towards, directions, act):
+        for d in directions:
+            dx, dy = DIRECTIONS[d]
+
+            @pl.when(exists(dx, dy) if towards else exists(-dx, -dy))
+            def _():
+                act(d)
+
+    def send_pair(phase, field, q):
+        for_existing(True, (0, 1), lambda d: pair_copy(phase, field, d, q).start())
+
+    def wait_pair(phase, field, q):
+        for_existing(False, (0, 1), lambda d: pair_copy(phase, field, d, q).wait_recv())
+
     def do_pack(phase, field):
         lane = lax.broadcasted_iota(jnp.int32, (nx, LANES), 1) // EDGE
         last = jnp.zeros((nx, LANES), F32)
@@ -194,68 +244,59 @@
             def _():
                 target[...] = jnp.zeros(target.shape, F32)
 
-    def send_halos(phase, field):
-        for d, (dx, dy) in enumerate(DIRECTIONS):
-
-            @pl.when(exists(dx, dy))
-            def _():
-                halo_copy(phase, field, d).start()
-
-    def wait_halos(phase, field):
-        for d, (dx, dy) in enumerate(DIRECTIONS):
-
-            @pl.when(exists(-dx, -dy))
-            def _():
-                halo_copy(phase, field, d).wait_recv()
+    others = range(2, 8)
+
+    def send_others(phase, field):
+        for_existing(True, others, lambda d: halo_copy(phase, field, d).start())
+
+    def wait_others(phase, field):
+        for_existing(False, others, lambda d: halo_copy(phase, field, d).wait_recv())
 
     def wait_sends(phase, field):
-        for d, (dx, dy) in enumerate(DIRECTIONS):
-
-            @pl.when(exists(dx, dy))
-            def _():
-                halo_copy(phase, field, d).wait_send()
-
-    def plane_copy(phase, z):
+        for_existing(True, others, lambda d: halo_copy(phase, field, d).wait_send())
+        for q in range(pairs):
+            for_existing(True, (0, 1), lambda d: pair_copy(phase, field, d, q).wait_send())
+            swap_copy(phase, q).wait_send()
+
+    def swap_copy(phase, q):
+        planes = pl.ds(2 * q, 2)
         return pltpu.make_async_remote_copy(
-            src_ref=own.at[phase, z],
-            dst_ref=peer.at[phase, z],
-            send_sem=es.at[phase, z],
-            recv_sem=er.at[phase, z],
+            src_ref=own.at[phase, planes],
+            dst_ref=peer.at[phase, planes],
+            send_sem=es.at[phase, q],
+            recv_sem=er.at[phase, q],
             device_id=partner,
             device_id_type=MESH,
         )
 
-    def forward(phase, field):
+    def forward(phase, field, q):
         lane = lax.broadcasted_iota(jnp.int32, (lx, LANES), 1)
-        for z in range(nz):
-            body = jnp.concatenate([xhalo[phase, 0, z], field[z], xhalo[phase, 1, z]], axis=0)
+        full = []
+        for z in (2 * q, 2 * q + 1):
+            rows = jnp.concatenate([xhalo[phase, 0, z], field[z], xhalo[phase, 1, z]], axis=0)
             left, right = yhalo[phase, 0], yhalo[phase, 1]
             if z:
                 left = pltpu.roll(left, LANES - EDGE * z, 1)
             if z != 1:
                 right = pltpu.roll(right, (EDGE - EDGE * z) % LANES, 1)
             side = jnp.where(lane < EDGE, left, jnp.where(lane < 2 * EDGE, right, 0.0))
-            full = jnp.concatenate([body, side], axis=1)
-            a_hi[z], a_lo[z] = split(full)
-        for z in range(nz):
-            hi = a_hi[z]
-            x1 = dot(hi, fy_hi[...]) + dot(a_lo[z], fy_hi[...]) + dot(hi, fy_lo[...])
-            hi, lo = split(x1)
-            d_hi[z, pl.ds(0, lx), :] = hi[:, :LANES]
-            d_hi[z, pl.ds(lx, lx), :] = hi[:, LANES:]
-            d_lo[z, pl.ds(0, lx), :] = lo[:, :LANES]
-            d_lo[z, pl.ds(lx, lx), :] = lo[:, LANES:]
-        for z in range(0, nz, 2):
-            hi = jnp.concatenate([d_hi[z], d_hi[z + 1]], axis=1)
-            lo = jnp.concatenate([d_lo[z], d_lo[z + 1]], axis=1)
-            both = dot(fx2[...], hi)
-            x2 = both[: 2 * lx] + both[2 * lx :] + dot(fx2[pl.ds(0, 2 * lx), :], lo)
-            own[phase, z] = x2[:, :LANES]
-            own[phase, z + 1] = x2[:, LANES:]
-            plane_copy(phase, z).start()
-            plane_copy(phase, z + 1).start()
-
-    def mix_planes(source, phase, base, conj, add):
+            full.append(jnp.concatenate([rows, side], axis=1))
+        hi, lo = split(jnp.concatenate(full, axis=0))
+        x1 = dot(hi, fy_hi[...]) + dot(lo, fy_hi[...]) + dot(hi, fy_lo[...])
+        stacked = [
+            jnp.concatenate(
+                [x1[k * lx : (k + 1) * lx, :LANES], x1[k * lx : (k + 1) * lx, LANES:]], axis=0
+            )
+            for k in range(2)
+        ]
+        hi, lo = split(jnp.concatenate(stacked, axis=1))
+        both = dot(fx2[...], hi)
+        x2 = both[: 2 * lx] + both[2 * lx :] + dot(fx2[pl.ds(0, 2 * lx), :], lo)
+        own[phase, 2 * q] = x2[:, :LANES]
+        own[phase, 2 * q + 1] = x2[:, LANES:]
+        swap_copy(phase, q).start()
+
+    def mix_planes(source, phase, base, conj, add, chosen):
         @pl.loop(0, lx // 8)
         def _(s):
             re = pl.ds(pl.multiple_of(s * 8, 8), 8)
@@ -263,10 +304,11 @@
             vr = [source[phase, j, re, :] for j in range(nz)]
             vi = [source[phase, j, im, :] for j in range(nz)]
             kr, ki = {}, {}
-            for d in range(1 - nz, nz):
+            reach = [(j - i if conj else i - j) for i in chosen for j in range(nz)]
+            for d in sorted(set(reach)):
                 kr[d] = k2[base + d, re, :]
                 ki[d] = k2[base + d, im, :]
-            for i in range(nz):
+            for i in chosen:
                 yr = mix[i, re, :] if add else None
                 yi = mix[i, im, :] if add else None
                 for j in range(nz):
@@ -279,8 +321,8 @@
                 mix[i, re, :] = yr
                 mix[i, im, :] = yi
 
-    def inverse(write):
-        for z in range(0, nz, 2):
+    def inverse(planes, write, after):
+        for z in planes:
             y = jnp.concatenate([mix[z], mix[z + 1]], axis=1)
             hi, lo = split(y)
             both = dot(ix2[...], hi)
@@ -293,24 +335,35 @@
                     z + k,
                     dot(hi, iy_hi[...]) + dot(lo, iy_hi[...]) + dot(hi, iy_lo[...]),
                 )
-
-    def convolve(phase, field, conj, write):
-        forward(phase, field)
+            after(z // 2)
+
+    def convolve(phase, field, conj, groups, write, after):
+        wait_others(phase, field)
+        for q in range(pairs):
+            wait_pair(phase, field, q)
+            forward(phase, field, q)
         sign = 1 - 2 * gz if conj else 2 * gz - 1
         middle = (extent - 1) // 2
-        mix_planes(own, phase, middle, conj, False)
-        for z in range(nz):
-            plane_copy(phase, z).wait_recv()
-        mix_planes(peer, phase, middle + sign * nz, conj, True)
-        inverse(write)
-
+        mix_planes(own, phase, middle, conj, False, range(nz))
+        for q in range(pairs):
+            swap_copy(phase, q).wait_recv()
+        size = nz // groups
+        for n in range(groups):
+            planes = range(n * size, (n + 1) * size)
+            mix_planes(peer, phase, middle + sign * nz, conj, True, planes)
+            inverse(planes[::2], write, after)
+
+    zero_missing(0)
+    loads[0].wait()
     do_pack(0, est_ref)
-    zero_missing(0)
     pl.semaphore_wait(barrier, chips)
-    send_halos(0, est_ref)
+    for q in range(pairs):
+        send_pair(0, est_ref, q)
+    send_others(0, est_ref)
     zero_missing(1)
 
-    psf_copy.wait()
+    for load in loads[1:]:
+        load.wait()
     chosen = psf[index_ref[0]]
     total = jnp.sum(chosen, axis=0)
     total = jnp.sum(jnp.sum(total, axis=1, keepdims=True), axis=0, keepdims=True)
@@ -339,21 +392,18 @@
             k2[n] = spectrum[:, :LANES]
             k2[n + 1] = spectrum[:, LANES:]
 
-    wait_halos(0, est_ref)
-
     def write_ratio(z, blurred):
         ratio[z] = view_ref[z] / blurred
 
-    convolve(0, est_ref, False, write_ratio)
+    convolve(0, est_ref, False, 2, write_ratio, lambda q: send_pair(1, ratio, q))
 
     do_pack(1, ratio)
-    send_halos(1, ratio)
-    wait_halos(1, ratio)
+    send_others(1, ratio)
 
     def write_update(z, correction):
         out_ref[z] = est_ref[z] * correction
 
-    convolve(1, ratio, True, write_update)
+    convolve(1, ratio, True, 1, write_update, lambda q: None)
 
     halves = [(out_ref[2 * i] + out_ref[2 * i + 1]) * 0.5 for i in range(nz // 2)]
     quarters = [(halves[2 * i] + halves[2 * i + 1]) * 0.5 for i in range(nz // 4)]
@@ -375,9 +425,6 @@
     share_copy.start()
     row, rows, col, cols = places[2]
     three_ref[0] = last[row : row + rows, col : col + cols]
-    row, rows, col, cols = places[0]
-    for i, plane in enumerate(halves):
-        one_ref[i] = pooled(plane)[row : row + rows, col : col + cols]
     row, rows, col, cols = places[1]
     for i, plane in enumerate(quarters):
         two_ref[i] = pooled(plane)[row : row + rows, col : col + cols]
@@ -408,10 +455,11 @@
     def _(offset):
         tile_copy(offset).start()
 
+    row, rows, col, cols = places[0]
+    for i, plane in enumerate(halves):
+        one_ref[i] = pooled(plane)[row : row + rows, col : col + cols]
     for phase, field in ((0, est_ref), (1, ratio)):
         wait_sends(phase, field)
-        for z in range(nz):
-            plane_copy(phase, z).wait_send()
 
     @pl.loop(1, chips)
     def _(offset):
@@ -421,6 +469,15 @@
     for offset in range(1, chips):
         five = five + tiles[offset]
     five_ref[0] = five[: five_ref.shape[1], : five_ref.shape[2]]
+
+
+def write_out(*refs):
+    sems = refs[12]
+    copies = [pltpu.make_async_copy(refs[i], refs[6 + i], sems.at[i]) for i in range(6)]
+    for copy in copies:
+        copy.start()
+    for copy in copies:
+        copy.wait()
 
 
 def local(sizes, estimate, view_data, psf_stack, view_index):
@@ -432,34 +489,30 @@
     wide = extent + 1
     chips = gxn * gyn
     vmem = pl.BlockSpec(memory_space=pltpu.VMEM)
+    hbm = pl.BlockSpec(memory_space=pltpu.HBM)
 
     def shape(*dims):
         return jax.ShapeDtypeStruct(dims, F32)
 
     rows5, cols5 = places[4][1] * gxn, places[4][3] * gyn
     dma = pltpu.SemaphoreType.DMA
-    return pl.pallas_call(
+    shapes = (
+        shape(nz, nx, ny),
+        shape(nz // 2, nx // 2, ny // 2),
+        shape(nz // 4, nx // 4, ny // 4),
+        shape(nz // 8, nx // 8, ny // 8),
+        shape(1, nx // 16, ny // 16),
+        shape(1, rows5, cols5),
+    )
+    results = pl.pallas_call(
         functools.partial(kernel, sizes, places),
-        out_shape=(
-            shape(nz, nx, ny),
-            shape(nz // 2, nx // 2, ny // 2),
-            shape(nz // 4, nx // 4, ny // 4),
-            shape(nz // 8, nx // 8, ny // 8),
-            shape(1, nx // 16, ny // 16),
-            shape(1, rows5, cols5),
-        ),
-        in_specs=[pl.BlockSpec(memory_space=pltpu.SMEM), vmem, vmem, pl.BlockSpec(memory_space=pl.ANY)]
-        + [vmem] * len(arrays),
+        out_shape=shapes,
+        in_specs=[pl.BlockSpec(memory_space=pltpu.SMEM)] + [hbm] * (len(arrays) + 3),
         out_specs=(vmem,) * 6,
         scratch_shapes=[
-            pltpu.VMEM(psf_stack.shape, F32),
             pltpu.VMEM((wide, wide, LANES), F32),
             pltpu.VMEM((wide, 6 * wide, LANES), BF),
             pltpu.VMEM((wide, 2 * lx, LANES), F32),
-            pltpu.VMEM((nz, lx, 2 * LANES), BF),
-            pltpu.VMEM((nz, lx, 2 * LANES), BF),
-            pltpu.VMEM((nz, 2 * lx, LANES), BF),
-            pltpu.VMEM((nz, 2 * lx, LANES), BF),
             pltpu.VMEM((2, nz, 2 * lx, LANES), F32),
             pltpu.VMEM((2, nz, 2 * lx, LANES), F32),
             pltpu.VMEM((nz, 2 * lx, LANES), F32),
@@ -470,21 +523,32 @@
             pltpu.VMEM((1, 8, LANES), F32),
             pltpu.VMEM((8, LANES), F32),
             pltpu.VMEM((chips, max(8, rows5), LANES), F32),
-            dma,
+            dma((len(arrays) + 3,)),
+            dma((2, 2, nz // 2)),
+            dma((2, 2, nz // 2)),
             dma((2, 8)),
             dma((2, 8)),
-            dma((2, nz)),
-            dma((2, nz)),
+            dma((2, nz // 2)),
+            dma((2, nz // 2)),
             dma,
             dma,
             dma((chips,)),
             dma((chips,)),
+            *[pltpu.VMEM(a.shape, a.dtype) for a in (estimate, psf_stack, *arrays, view_data)],
         ],
         compiler_params=pltpu.CompilerParams(
-            collective_id=0, has_side_effects=True, vmem_limit_bytes=48 * 1024 * 1024
+            collective_id=0, has_side_effects=True, vmem_limit_bytes=67043328 - 450000
         ),
         name="deconvolve",
     )(view_index, estimate, view_data, psf_stack, *[jnp.asarray(a) for a in arrays])
+    return pl.pallas_call(
+        write_out,
+        out_shape=shapes,
+        in_specs=[vmem] * 6,
+        out_specs=(hbm,) * 6,
+        scratch_shapes=[dma((6,))],
+        name="write_out",
+    )(*results)
 
 
 def solution(mesh):

time: 52 us -> 38.1 us (0.73)
  local copies, waits for them, and re-layouts: 16.8 us -> 0 us
  Pallas kernels: 33.2 us -> 36.6 us
    unnamed x34 -> x0, local copies, waits for them, and re-layouts: 16.8 us -> none
    pallas_call x1 -> x2, Pallas kernels: 33.2 us -> 36.6 us  [the longest x1 34.8 us: local(): pl.pallas_call(functools.partial(kernel, sizes, places), out_shape=shapes...]
where the time goes in v1:
time: 38.1 us; the launch traced here: 37.9 us
  Pallas kernels  36.6 us (96%)
  between operations  1.29 us (3%)
    pallas_call x1, Pallas kernels, local(): pl.pallas_call(functools.partial(kernel, sizes, places), out_shape=shapes...  34.8 us
    pallas_call x1, Pallas kernels, local(): pl.pallas_call(write_out, out_shape=shapes, in_specs=[vmem] * 6, out_spec...  1.78 us

profile of v1, /device:TPU:0, one launch (start us, length us, event | category | flops | bytes accessed | tf_op | source)
XLA Modules:
  0.0 37.9 jit_solution(10448763806621132609)
XLA Ops:
  1.3 34.8 %deconvolve.1 = (f32[8,64,128]{2,1,0:T(8,128)}, f32[4,32,64]{2,1,0:T(8,128)}, f32[2,16,32]{2,1,0:T(8,128)}, f32[1,8,16]{2,1,0:T(8,128)}, f32[1,4,8]{2,1,0:T(4,128)}, /*index=5*/f32[1,8,16]{2,1,0:T(8,128)}) custom-call(s32[1]{0:T(128)S(6)} %copy.21.index_ref, f32[8,64,128]{2,1,0:T(8,128)} %est_hbm.1, f32[8,64,128]{2,1,0:T(8,128)} %view_hbm.1, ...), custom_call_target="tpu_custom_call" | custom-call | tf_op jit(solution)/shard_map/deconvolve/pallas_call | solution.py:507
  36.1 1.8 %write_out.1 = (f32[8,64,128]{2,1,0:T(8,128)}, f32[4,32,64]{2,1,0:T(8,128)}, f32[2,16,32]{2,1,0:T(8,128)}, f32[1,8,16]{2,1,0:T(8,128)}, f32[1,4,8]{2,1,0:T(4,128)}, /*index=5*/f32[1,8,16]{2,1,0:T(8,128)}) custom-call(f32[8,64,128]{2,1,0:T(8,128)} %get-tuple-element.12.refs_0_, f32[4,32,64]{2,1,0:T(8,128)} %get-tuple-element.13.refs_1_, ...), custom_call_target="tpu_custom_call" | custom-call | tf_op jit(solution)/shard_map/write_out/pallas_call | solution.py:544

commit v2 on v1

--- a/solution.py
+++ b/solution.py
@@ -308,18 +308,20 @@
             for d in sorted(set(reach)):
                 kr[d] = k2[base + d, re, :]
                 ki[d] = k2[base + d, im, :]
+            ks = {d: kr[d] - ki[d] if conj else kr[d] + ki[d] for d in kr}
+            vs = [r + i for r, i in zip(vr, vi)]
             for i in chosen:
-                yr = mix[i, re, :] if add else None
-                yi = mix[i, im, :] if add else None
+                a = b = c = None
                 for j in range(nz):
                     d = j - i if conj else i - j
-                    rr, ii = kr[d] * vr[j], ki[d] * vi[j]
-                    ri, ir = kr[d] * vi[j], ki[d] * vr[j]
-                    tr, ti = (rr + ii, ri - ir) if conj else (rr - ii, ri + ir)
-                    yr = tr if yr is None else yr + tr
-                    yi = ti if yi is None else yi + ti
-                mix[i, re, :] = yr
-                mix[i, im, :] = yi
+                    rr, ii, ss = kr[d] * vr[j], ki[d] * vi[j], ks[d] * vs[j]
+                    a = rr if a is None else a + rr
+                    b = ii if b is None else b + ii
+                    c = ss if c is None else c + ss
+                yr = a + b if conj else a - b
+                yi = c - a + b if conj else c - a - b
+                mix[i, re, :] = mix[i, re, :] + yr if add else yr
+                mix[i, im, :] = mix[i, im, :] + yi if add else yi
 
     def inverse(planes, write, after):
         for z in planes:

time: 38.1 us -> 37.9 us (level)
  no operation moved by 1% of the time
where the time goes in v2:
time: 37.9 us; the launch traced here: 37.8 us
  Pallas kernels  36.5 us (96%)
  between operations  1.29 us (3%)
    pallas_call x1, Pallas kernels, local(): pl.pallas_call(functools.partial(kernel, sizes, places), out_shape=shapes...  34.7 us
    pallas_call x1, Pallas kernels, local(): pl.pallas_call(write_out, out_shape=shapes, in_specs=[vmem] * 6, out_spec...  1.78 us

profile of v2, /device:TPU:0, one launch (start us, length us, event | category | flops | bytes accessed | tf_op | source)
XLA Modules:
  0.0 37.8 jit_solution(13812907665553103026)
XLA Ops:
  1.3 34.7 %deconvolve.1 = (f32[8,64,128]{2,1,0:T(8,128)}, f32[4,32,64]{2,1,0:T(8,128)}, f32[2,16,32]{2,1,0:T(8,128)}, f32[1,8,16]{2,1,0:T(8,128)}, f32[1,4,8]{2,1,0:T(4,128)}, /*index=5*/f32[1,8,16]{2,1,0:T(8,128)}) custom-call(s32[1]{0:T(128)S(6)} %copy.21.index_ref, f32[8,64,128]{2,1,0:T(8,128)} %est_hbm.1, f32[8,64,128]{2,1,0:T(8,128)} %view_hbm.1, ...), custom_call_target="tpu_custom_call" | custom-call | tf_op jit(solution)/shard_map/deconvolve/pallas_call | solution.py:509
  36.0 1.8 %write_out.1 = (f32[8,64,128]{2,1,0:T(8,128)}, f32[4,32,64]{2,1,0:T(8,128)}, f32[2,16,32]{2,1,0:T(8,128)}, f32[1,8,16]{2,1,0:T(8,128)}, f32[1,4,8]{2,1,0:T(4,128)}, /*index=5*/f32[1,8,16]{2,1,0:T(8,128)}) custom-call(f32[8,64,128]{2,1,0:T(8,128)} %get-tuple-element.12.refs_0_, f32[4,32,64]{2,1,0:T(8,128)} %get-tuple-element.13.refs_1_, ...), custom_call_target="tpu_custom_call" | custom-call | tf_op jit(solution)/shard_map/write_out/pallas_call | solution.py:546
